TPU v7x, 32 devices: a whole 2x2x4 slice. The times are simulated.
32 devices in a mesh: inst: 4 (over x, core), shard: 8 (over z, y).
Axes of the slice: x: 2, y: 2, z: 4, core: 2. Of those that a mesh axis runs over, the one named last changes fastest.
Arguments:
- tokens: bfloat16 [2048, 5120], P(('inst', 'shard')), may hold values from -600 to 600
- norm_gain: float32 [5120], P(('inst', 'shard')), may hold values from 0.1 to 1.9
- master_qkv: float32 [5120, 7168], P(('inst', 'shard')), may hold values from -0.078125 to 0.078125
- qkv_bias: float32 [7168], P(('inst', 'shard')), may hold values from -3 to 3
Outputs:
- qkv_out: bfloat16 [32, 512, 896], P(('inst', 'shard'))
All inputs are finite; a program needn't handle non-finite values.
Results may differ from a plain program's by a relative error of at most 0.0062.
Values may be sent and summed in bfloat16 or wider, within the bound.
A program may use at most 64 MiB of HBM per device.

v0:
```python
import jax
import jax.numpy as jnp
from jax import lax
from jax.sharding import PartitionSpec as P

QHEADS = 40
KVHEADS = 8
HEAD_DIM = 128
TP = 8


EPSILON = 1e-06


def partner_2(value, axis, distance):
    mask = 2**distance
    pairs = [(source, source ^ mask) for source in range(lax.axis_size(axis))]
    return lax.ppermute(value, axis, pairs)


def rank_columns(matrix):
    query_cols = QHEADS * HEAD_DIM
    pair_cols = KVHEADS * HEAD_DIM
    leading = matrix.shape[:-1]
    query = matrix[..., :query_cols].reshape(leading + (TP, query_cols // TP))
    keys = matrix[..., query_cols : query_cols + pair_cols].reshape(leading + (TP, pair_cols // TP))
    values = matrix[..., query_cols + pair_cols :].reshape(leading + (TP, pair_cols // TP))
    return jnp.concatenate([query, keys, values], axis=-1)


def normalize(tokens, gain):
    floats = tokens.astype(jnp.float32)
    scale = lax.rsqrt(jnp.mean(floats * floats, axis=-1, keepdims=True) + EPSILON)
    return (floats * scale * gain.astype(jnp.float32)).astype(jnp.bfloat16)


def per_device(tokens, norm_gain, master_qkv, qkv_bias):
    shard_count = lax.axis_size("shard")
    local_rows = master_qkv.shape[0]
    rank_width = master_qkv.shape[1] // TP
    gain_full, bias_full = (
        lax.all_gather(norm_gain.astype(jnp.bfloat16), ("inst", "shard"), axis=0, tiled=True),
        lax.all_gather(qkv_bias.astype(jnp.bfloat16), ("inst", "shard"), axis=0, tiled=True),
    )
    normed = normalize(tokens, gain_full)
    shard_pos = lax.axis_index("shard")
    rank_index = shard_pos % TP
    bit_count = TP.bit_length() - 1
    bit_order = list(range(bit_count))
    group_rows = normed
    for bit_pos in bit_order:
        partner = partner_2(group_rows, "shard", bit_pos)
        lower = jnp.bitwise_and(jnp.right_shift(shard_pos, bit_pos), 1) == 0
        group_rows = jnp.where(
            lower,
            jnp.concatenate([group_rows, partner], 0),
            jnp.concatenate([partner, group_rows], 0),
        )
    copies = shard_count // TP
    inst_block = shard_count * local_rows
    rows_low = master_qkv.astype(jnp.bfloat16)
    ranked = jnp.transpose(rank_columns(rows_low), (1, 0, 2))
    spread = jnp.broadcast_to(ranked[None], (copies,) + ranked.shape)
    outgoing = spread.reshape(shard_count, rows_low.shape[0], rank_width)
    arrived = lax.all_to_all(outgoing, "shard", split_axis=0, concat_axis=0, tiled=True).reshape(
        inst_block, rank_width
    )
    product = jnp.dot(
        group_rows,
        lax.all_gather(arrived, "inst", axis=0, tiled=True),
        preferred_element_type=jnp.float32,
    )
    bias_ranks = rank_columns(bias_full)
    bias_mine = lax.dynamic_index_in_dim(bias_ranks, rank_index, 0, keepdims=False)
    result = (product + bias_mine.astype(jnp.float32)).astype(jnp.bfloat16)
    return result[None]


def solution(mesh):
    in_specs = (
        P(("inst", "shard"), None),
        P(("inst", "shard")),
        P(("inst", "shard"), None),
        P(("inst", "shard")),
    )
    out_specs = P(("inst", "shard"), None, None)
    return jax.shard_map(
        per_device, mesh=mesh, in_specs=in_specs, out_specs=out_specs, check_vma=False
    )
```

profile of v0, /device:TPU:0, one launch (start us, length us, event | category | flops | bytes accessed | tf_op | source)
XLA Modules:
  0.0 292.7 jit_solution(10127492376784495317)
XLA Ops:
  6.5 0.0 all-gather.2.cloned.1.call-start
  6.5 2.6 convert_element_type.27
  9.2 0.1 slice.46
  9.3 0.3 copy.7
  9.6 0.1 copy.8
  9.6 0.1 copy.9
  9.7 0.2 maximum_bitcast_fusion
  9.9 0.3 copy.6
  10.2 0.0 copy-start.1
  10.2 0.0 copy-start.2
  10.2 0.0 copy-start
  10.3 59.9 %all_to_all.5 = bf16[8,160,896]{2,1,0:T(8,128)(2,1)} all-to-all(bf16[8,160,896]{2,1,0:T(8,128)(2,1)S(1)} %copy.6), channel_id=1, replica_groups=mesh['inst'=4,'shard'=8] {'shard'}, dimensions={0} | all-to-all | bytes 4587520 | tf_op jit(solution)/shard_map/all_to_all | solution.py:65
  70.1 0.0 all-gather.2.cloned.1.call-update
  70.1 0.0 copy-done.1
  70.2 0.0 copy-done.2
  70.2 0.2 dynamic-update-slice
  70.5 0.2 dynamic-update-slice.1
  70.7 40.0 %all-reduce.2 = (bf16[5120]{0:T(1024)(128)(2,1)S(1)}, bf16[7168]{0:T(1024)(128)(2,1)S(1)}) all-reduce(bf16[5120]{0:T(1024)(128)(2,1)S(1)} %dynamic-update-slice, bf16[7168]{0:T(1024)(128)(2,1)S(1)} %dynamic-update-slice.1), channel_id=1, replica_groups=mesh['inst'=4,'shard'=8] {'inst','shard'}, use_global_device_ids=true, to_apply=%add | all-reduce | flops 12288 | bytes 49152
  110.6 0.0 copy-done
  110.6 0.2 fusion.8
  110.9 0.2 fusion.10
  111.1 2.4 collective-permute-start
  113.5 14.4 %collective-permute-done = bf16[64,5120]{1,0:T(8,128)(2,1)S(1)} collective-permute-done((bf16[64,5120]{1,0:T(8,128)(2,1)S(1)}, bf16[64,5120]{1,0:T(8,128)(2,1)S(1)}, u32[]{:S(2)}, u32[]{:S(2)}) %collective-permute-start) | collective-permute-done | bytes 655392 | tf_op jit(solution)/shard_map/ppermute | solution.py:18
  127.9 0.3 maximum_select_fusion.7
  128.1 1.8 collective-permute-start.1
  129.9 27.9 %collective-permute-done.1 = bf16[128,5120]{1,0:T(8,128)(2,1)S(1)} collective-permute-done((bf16[128,5120]{1,0:T(8,128)(2,1)S(1)}, bf16[128,5120]{1,0:T(8,128)(2,1)S(1)}, u32[]{:S(2)}, u32[]{:S(2)}) %collective-permute-start.1) | collective-permute-done | bytes 1310752 | tf_op jit(solution)/shard_map/ppermute | solution.py:18
  157.9 2.0 maximum_select_fusion.2
  159.9 1.8 collective-permute-start.2
  161.8 112.3 %collective-permute-done.2 = bf16[256,5120]{1,0:T(8,128)(2,1)S(1)} collective-permute-done((bf16[256,5120]{1,0:T(8,128)(2,1)}, bf16[256,5120]{1,0:T(8,128)(2,1)S(1)}, u32[]{:S(2)}, u32[]{:S(2)}) %collective-permute-start.2) | collective-permute-done | bytes 2621472 | tf_op jit(solution)/shard_map/ppermute | solution.py:18
  274.1 0.0 all-gather.2.cloned.1.call-done
  274.1 11.8 %fusion.7 = bf16[1,512,896]{2,1,0:T(8,128)(2,1)} fusion(bf16[5120,896]{1,0:T(8,128)(2,1)} %all-gather.2.cloned.1.call-done, bf16[256,5120]{1,0:T(8,128)(2,1)S(1)} %collective-permute-done.2, bf16[256,5120]{1,0:T(8,128)(2,1)} %maximum_select_fusion.2, pred[]{:T(512)S(6)} %eq.11, f32[896]{0:T(1024)S(1)} %convert_reduce_fusion), kind=kOutput, calls=%fused_computation.13 | convolution fusion | flops 4722130944 | bytes 15339009 | tf_op jit(solution)/shard_map/dot_general | solution.py:68
  (11 shorter events, 0.1 us)
Async XLA Ops:
  6.5 267.6 %all-gather.2.cloned.1.call-start = ((), (), s32[]{:S(2)}) async-start(), calls=%async_computation.1 | async-start | bytes 11468800 | tf_op jit(solution)/shard_map/all_gather | solution.py:70
  10.2 59.9 %copy-start.1 = (f32[160]{0:T(256)S(1)}, f32[160]{0:T(256)}, u32[]{:S(2)}) copy-start(f32[160]{0:T(256)} %param.5) | copy-start | bytes 1924
  10.2 59.9 %copy-start.2 = (f32[224]{0:T(256)S(1)}, f32[224]{0:T(256)}, u32[]{:S(2)}) copy-start(f32[224]{0:T(256)} %param.7) | copy-start | bytes 2692
  10.2 100.4 %copy-start = (bf16[64,5120]{1,0:T(8,128)(2,1)S(1)}, bf16[64,5120]{1,0:T(8,128)(2,1)}, u32[]{:S(2)}) copy-start(bf16[64,5120]{1,0:T(8,128)(2,1)} %param.4) | copy-start | bytes 1966084
  111.1 16.7 %collective-permute-start = (bf16[64,5120]{1,0:T(8,128)(2,1)S(1)}, bf16[64,5120]{1,0:T(8,128)(2,1)S(1)}, u32[]{:S(2)}, u32[]{:S(2)}) collective-permute-start(bf16[64,5120]{1,0:T(8,128)(2,1)S(1)} %fusion.10), channel_id=1, source_target_pairs={{0,1},{1,0},{2,3},{3,2},{4,5},{5,4},{6,7},{7,6},{8,9},{9,8},{10,11... | collective-permute-start | bytes 1966088 | tf_op jit(solution)/shard_map/ppermute | solution.py:18
  128.1 29.8 %collective-permute-start.1 = (bf16[128,5120]{1,0:T(8,128)(2,1)S(1)}, bf16[128,5120]{1,0:T(8,128)(2,1)S(1)}, u32[]{:S(2)}, u32[]{:S(2)}) collective-permute-start(bf16[128,5120]{1,0:T(8,128)(2,1)S(1)} %maximum_select_fusion.7), channel_id=1, source_target_pairs={{0,2},{1,3},{2,0},{3,1},{4,6},{5,7},{6,4},{7,5},{8,10},{9,11},{10,... | collective-permute-start | bytes 3932168 | tf_op jit(solution)/shard_map/ppermute | solution.py:18
  159.9 114.2 %collective-permute-start.2 = (bf16[256,5120]{1,0:T(8,128)(2,1)}, bf16[256,5120]{1,0:T(8,128)(2,1)S(1)}, u32[]{:S(2)}, u32[]{:S(2)}) collective-permute-start(bf16[256,5120]{1,0:T(8,128)(2,1)} %maximum_select_fusion.2), channel_id=1, source_target_pairs={{0,4},{1,5},{2,6},{3,7},{4,0},{5,1},{6,2},{7,3},{8,12},{9,13},{10,... | collective-permute-start | bytes 7864328 | tf_op jit(solution)/shard_map/ppermute | solution.py:18
Sparse Core Ops, SparseCore 0:
  70.3 62.5 all-gather.1
where the time goes:
time: 293 us
  waiting for transfers between devices  155 us (53%)
  blocking collectives  99.8 us (34%)
  between operations  13.6 us (5%)
  matrix products  11.8 us (4%)
  starting transfers between devices  6 us (2%)
  other arithmetic  5.53 us (2%)
    ppermute x3, waiting for transfers between devices, partner_2(): return lax.ppermute(value, axis, pairs)  155 us
    all_to_all x1, blocking collectives, per_device(): lax.all_to_all(outgoing, 'shard', split_axis=0, concat_axis=0, tiled=True)  59.9 us
    unnamed x1, blocking collectives  40 us
    dot_general x1, matrix products, per_device(): jnp.dot(group_rows, lax.all_gather(arrived, 'inst', axis=0, tiled=True),...  11.8 us
    ppermute x3, starting transfers between devices, partner_2(): return lax.ppermute(value, axis, pairs)  6 us
  transfers between devices with their start and end apart: 4, of which 3 were waited for; matrix products, arithmetic and copies ran while one was open for 1% of the time, Pallas kernels for 0%

commit v1 on v0

--- a/solution.py
+++ b/solution.py
@@ -1,6 +1,10 @@
+import functools
+
 import jax
 import jax.numpy as jnp
 from jax import lax
+from jax.experimental import pallas as pl
+from jax.experimental.pallas import tpu as pltpu
 from jax.sharding import PartitionSpec as P
 
 QHEADS = 40
@@ -10,6 +14,9 @@
 
 
 EPSILON = 1e-06
+MESH = pl.DeviceIdType.MESH
+LANES = 128
+TOKEN_PIECES = 2
 
 
 def partner_2(value, axis, distance):
@@ -34,7 +41,7 @@
     return (floats * scale * gain.astype(jnp.float32)).astype(jnp.bfloat16)
 
 
-def per_device(tokens, norm_gain, master_qkv, qkv_bias):
+def general_device(tokens, norm_gain, master_qkv, qkv_bias):
     shard_count = lax.axis_size("shard")
     local_rows = master_qkv.shape[0]
     rank_width = master_qkv.shape[1] // TP
@@ -76,6 +83,345 @@
     return result[None]
 
 
+def kernel(
+    dims,
+    tok_ref,
+    gain_ref,
+    w_ref,
+    bias_ref,
+    out_ref,
+    tbuf,
+    wbuf,
+    wsend,
+    bbuf,
+    scale_ref,
+    t_recv,
+    t_send,
+    w_recv,
+    a_send,
+    x_send,
+    d_send,
+    b_recv,
+    b_send,
+):
+    inst_count, shard_count, group = dims
+    devices = inst_count * shard_count
+    line = shard_count // 2
+    inst = lax.axis_index("inst")
+    me = lax.axis_index("shard")
+    z = me // 2
+    y = lax.rem(me, 2)
+    flat = inst * shard_count + me
+    core_peer = inst + 1 - 2 * lax.rem(inst, 2)
+    x_peer = lax.rem(inst + 2, inst_count)
+    y_peer = z * 2 + 1 - y
+    rows = w_ref.shape[0]
+    width = wsend.shape[2]
+    pieces = TOKEN_PIECES
+    piece_rows = tok_ref.shape[0] // pieces
+
+    def mate(k):
+        dy, dz = k % 2, k // 2
+        zz = z if dz == 0 else (z + 1 - 2 * lax.rem(z, 2), lax.rem(z + 2, line), line - 1 - z)[dz - 1]
+        return zz * 2 + lax.rem(y + dy, 2)
+
+    barrier = pltpu.get_barrier_semaphore()
+
+    @pl.loop(1, devices)
+    def _(step):
+        there = lax.rem(flat + step, devices)
+        pl.semaphore_signal(
+            barrier,
+            inc=1,
+            device_id=(there // shard_count, lax.rem(there, shard_count)),
+            device_id_type=MESH,
+        )
+
+    gain = gain_ref[...].astype(jnp.bfloat16).astype(jnp.float32)
+    query = QHEADS * HEAD_DIM // TP
+    pair = KVHEADS * HEAD_DIM // TP
+    for rank in range(TP):
+        starts = (
+            (rank * query, 0, query),
+            (TP * query + rank * pair, query, pair),
+            (TP * (query + pair) + rank * pair, query + pair, pair),
+        )
+        for source, target, extent in starts:
+            part = w_ref[:, source : source + extent].astype(jnp.bfloat16).astype(jnp.float32)
+            wsend[rank, :, target : target + extent] = (part * gain).astype(jnp.bfloat16)
+    for piece in range(pieces):
+        tbuf[me * pieces + piece] = tok_ref[piece * piece_rows : (piece + 1) * piece_rows, :]
+    bbuf[flat] = bias_ref[...]
+    pl.semaphore_wait(barrier, devices - 1)
+
+    def token_copy(block, piece, way, target):
+        index = block * pieces + piece
+        return pltpu.make_async_remote_copy(
+            src_ref=tbuf.at[index],
+            dst_ref=tbuf.at[index],
+            send_sem=t_send.at[way, index],
+            recv_sem=t_recv.at[index],
+            device_id=(inst, target),
+            device_id_type=MESH,
+        )
+
+    def own_token_copy(piece, way, target):
+        index = me * pieces + piece
+        return pltpu.make_async_remote_copy(
+            src_ref=tok_ref.at[pl.ds(piece * piece_rows, piece_rows)],
+            dst_ref=tbuf.at[index],
+            send_sem=t_send.at[way, index],
+            recv_sem=t_recv.at[index],
+            device_id=(inst, target),
+            device_id_type=MESH,
+        )
+
+    def weight_copy(source, target, slot, send_sem):
+        return pltpu.make_async_remote_copy(
+            src_ref=source,
+            dst_ref=wbuf.at[slot],
+            send_sem=send_sem,
+            recv_sem=w_recv.at[slot],
+            device_id=target,
+            device_id_type=MESH,
+        )
+
+    def all_gather_copy(k):
+        there = mate(k)
+        return weight_copy(wsend.at[there], (inst, there), flat, a_send.at[k])
+
+    def x_copy(k):
+        slot = inst * shard_count + mate(k)
+        source = wsend.at[me] if k == 0 else wbuf.at[slot]
+        return weight_copy(source, (x_peer, me), slot, x_send.at[k])
+
+    def core_copy(k, owner, side):
+        slot = owner * shard_count + mate(k)
+        source = wsend.at[me] if k == 0 and side == 0 else wbuf.at[slot]
+        return weight_copy(source, (core_peer, me), slot, d_send.at[side, k])
+
+    up = lax.rem(z + 1, line) * 2 + y
+    down = lax.rem(z + line - 1, line) * 2 + y
+
+    def each(condition, action):
+        pl.when(condition)(action)
+
+    for piece in range(pieces):
+        each(z < line - 1, lambda piece=piece: own_token_copy(piece, 0, up).start())
+        each(z > 0, lambda piece=piece: own_token_copy(piece, 1, down).start())
+        own_token_copy(piece, 2, y_peer).start()
+    core_copy(0, inst, 0).start()
+    x_copy(0).start()
+    order = (7, 6, 5, 4, 3, 2, 1)
+    for k in order:
+        all_gather_copy(k).start()
+
+    def bias_copy(step):
+        there = lax.rem(flat + step, devices)
+        return pltpu.make_async_remote_copy(
+            src_ref=bias_ref,
+            dst_ref=bbuf.at[flat],
+            send_sem=b_send.at[step],
+            recv_sem=b_recv.at[flat],
+            device_id=(there // shard_count, lax.rem(there, shard_count)),
+            device_id_type=MESH,
+        )
+
+    @pl.loop(1, devices)
+    def _(step):
+        bias_copy(step).start()
+
+    wbuf[flat] = wsend[me]
+
+    def wait_block(slot):
+        pltpu.make_async_copy(wbuf.at[slot], wbuf.at[slot], w_recv.at[slot]).wait()
+
+    def wait_token(block, piece):
+        index = block * pieces + piece
+        pltpu.make_async_copy(tbuf.at[index], tbuf.at[index], t_recv.at[index]).wait()
+
+    def relay_token(distance, piece):
+        def from_below():
+            block = (z - distance) * 2 + y
+            wait_token(block, piece)
+            each(z < line - 1, lambda: token_copy(block, piece, 0, up).start())
+            token_copy(block, piece, 2, y_peer).start()
+
+        def from_above():
+            block = (z + distance) * 2 + y
+            wait_token(block, piece)
+            each(z > 0, lambda: token_copy(block, piece, 1, down).start())
+            token_copy(block, piece, 2, y_peer).start()
+
+        each(z >= distance, from_below)
+        each(z + distance < line, from_above)
+
+    def relay_weight(k):
+        wait_block(inst * shard_count + mate(k))
+        x_copy(k).start()
+        core_copy(k, inst, 0).start()
+
+    def relay_x(k):
+        wait_block(x_peer * shard_count + mate(k))
+        core_copy(k, x_peer, 1).start()
+
+    def relay_hop(distance):
+        for piece in range(pieces):
+            relay_token(distance, piece)
+
+    def scale_of(index):
+        values = tbuf[index].astype(jnp.float32)
+        mean = jnp.sum(values * values, axis=-1, keepdims=True) * (1.0 / tok_ref.shape[1])
+        scale_ref[pl.ds(pl.multiple_of(index * piece_rows, piece_rows), piece_rows), :] = jnp.broadcast_to(
+            lax.rsqrt(mean + EPSILON), (piece_rows, LANES)
+        )
+
+    relay_hop(1)
+    relay_x(0)
+    for k in order[:3]:
+        relay_weight(k)
+    relay_hop(2)
+    for k in order[3:5]:
+        relay_weight(k)
+    for k in order[:2]:
+        relay_x(k)
+    relay_hop(3)
+    for k in order[5:]:
+        relay_weight(k)
+    for k in order[2:]:
+        relay_x(k)
+
+    for k in range(shard_count):
+        wait_block(core_peer * shard_count + mate(k))
+        wait_block(lax.rem(core_peer + 2, inst_count) * shard_count + mate(k))
+    for block_z in range(line):
+        for piece in range(pieces):
+            wait_token(block_z * 2 + 1 - y, piece)
+
+    @pl.loop(0, shard_count * pieces)
+    def _(index):
+        scale_of(index)
+
+    @pl.loop(1, devices)
+    def _(step):
+        slot = lax.rem(flat + step, devices)
+        pltpu.make_async_copy(bbuf.at[slot], bbuf.at[slot], b_recv.at[slot]).wait()
+
+    per_row = LANES // group
+    held = bias_ref.shape[0]
+    lane = lax.broadcasted_iota(jnp.int32, (1, LANES), 1) // group
+
+    def bias_row(first):
+        row = jnp.zeros((1, LANES), jnp.float32)
+        for j in range(per_row):
+            number = first + j
+            row = jnp.where(lane == j, bbuf[number // held, pl.ds(lax.rem(number, held), 1), :], row)
+        return row.astype(jnp.bfloat16).astype(jnp.float32)
+
+    tile = 2 * LANES
+    depth = devices * rows
+    scale = scale_ref[...]
+    for start in range(0, width, tile):
+        extent = min(tile, width - start)
+        product = jnp.dot(
+            tbuf[...].reshape(shard_count * pieces * piece_rows, depth),
+            wbuf[:, :, start : start + extent].reshape(depth, extent),
+            preferred_element_type=jnp.float32,
+        )
+        for inner in range(0, extent, LANES):
+            at = start + inner
+            if at < query:
+                column = me * query + at
+            elif at < query + pair:
+                column = TP * query + me * pair + (at - query)
+            else:
+                column = TP * (query + pair) + me * pair + (at - query - pair)
+            out_ref[0, :, at : at + LANES] = (
+                product[:, inner : inner + LANES] * scale + bias_row(column // group)
+            ).astype(jnp.bfloat16)
+
+    for piece in range(pieces):
+        each(z < line - 1, lambda piece=piece: own_token_copy(piece, 0, up).wait_send())
+        each(z > 0, lambda piece=piece: own_token_copy(piece, 1, down).wait_send())
+        own_token_copy(piece, 2, y_peer).wait_send()
+        for distance in range(1, line):
+
+            def below(piece=piece, distance=distance):
+                block = (z - distance) * 2 + y
+                each(z < line - 1, lambda: token_copy(block, piece, 0, up).wait_send())
+                token_copy(block, piece, 2, y_peer).wait_send()
+
+            def above(piece=piece, distance=distance):
+                block = (z + distance) * 2 + y
+                each(z > 0, lambda: token_copy(block, piece, 1, down).wait_send())
+                token_copy(block, piece, 2, y_peer).wait_send()
+
+            each(z >= distance, below)
+            each(z + distance < line, above)
+    for k in range(shard_count):
+        if k:
+            all_gather_copy(k).wait_send()
+        x_copy(k).wait_send()
+        core_copy(k, inst, 0).wait_send()
+        core_copy(k, x_peer, 1).wait_send()
+
+    @pl.loop(1, devices)
+    def _(step):
+        bias_copy(step).wait_send()
+
+
+def kernel_device(dims, tokens, norm_gain, master_qkv, qkv_bias):
+    inst_count, shard_count, group = dims
+    devices = inst_count * shard_count
+    rows = master_qkv.shape[0]
+    width = master_qkv.shape[1] // TP
+    pieces = TOKEN_PIECES
+    groups = qkv_bias.shape[0] // group
+    bias = jnp.tile(qkv_bias.reshape(groups, group), (1, LANES // group))
+    index_count = shard_count * pieces
+    dma = pltpu.SemaphoreType.DMA
+    vmem = pl.BlockSpec(memory_space=pltpu.VMEM)
+    return pl.pallas_call(
+        functools.partial(kernel, dims),
+        out_shape=jax.ShapeDtypeStruct((1, shard_count * tokens.shape[0], width), jnp.bfloat16),
+        in_specs=[vmem] * 4,
+        out_specs=vmem,
+        scratch_shapes=[
+            pltpu.VMEM((index_count, tokens.shape[0] // pieces, tokens.shape[1]), jnp.bfloat16),
+            pltpu.VMEM((devices, rows, width), jnp.bfloat16),
+            pltpu.VMEM((TP, rows, width), jnp.bfloat16),
+            pltpu.VMEM((devices, groups, LANES), jnp.float32),
+            pltpu.VMEM((shard_count * tokens.shape[0], LANES), jnp.float32),
+            dma((index_count,)),
+            dma((3, index_count)),
+            dma((devices,)),
+            dma((shard_count,)),
+            dma((shard_count,)),
+            dma((2, shard_count)),
+            dma((devices,)),
+            dma((devices,)),
+        ],
+        compiler_params=pltpu.CompilerParams(
+            collective_id=0, has_side_effects=True, vmem_limit_bytes=60 * 1024 * 1024
+        ),
+    )(tokens, norm_gain.reshape(rows, 1), master_qkv, bias)
+
+
+def per_device(tokens, norm_gain, master_qkv, qkv_bias):
+    inst_count, shard_count = lax.axis_size("inst"), lax.axis_size("shard")
+    group = 32
+    fits = (
+        shard_count == TP
+        and inst_count == 4
+        and master_qkv.shape[0] % 16 == 0
+        and tokens.shape[0] % (16 * TOKEN_PIECES) == 0
+        and qkv_bias.shape[0] % group == 0
+    )
+    if fits:
+        return kernel_device((inst_count, shard_count, group), tokens, norm_gain, master_qkv, qkv_bias)
+    return general_device(tokens, norm_gain, master_qkv, qkv_bias)
+
+
 def solution(mesh):
     in_specs = (
         P(("inst", "shard"), None),

time: 293 us -> 137 us (0.47)
  the two profiles are of different devices: /device:TPU:0 before, /device:TPU:11 now
where the time goes in v1:
time: 137 us; the launch traced here: 136 us
  Pallas kernels  131 us (96%)
  local copies, waits for them, and re-layouts  5.03 us (4%)
    pallas_call x1, Pallas kernels, kernel_device(): pl.pallas_call(functools.partial(kernel, dims), out_shape=jax.ShapeDtypeS...  131 us

profile of v1, /device:TPU:11, one launch (start us, length us, event | category | flops | bytes accessed | tf_op | source)
XLA Modules:
  0.0 136.4 jit_solution(8197709275825335753)
XLA Ops:
  0.0 0.8 tile.10
  0.8 0.7 tile.12.bias_ref
  1.4 1.4 %copy.5.gain_ref = f32[160,1]{1,0:T(8,128)} copy(f32[160,1]{0,1:T(1,128)} %bitcast.1) | data formatting | bytes 1280 | tf_op jit(solution)/shard_map/reshape | solution.py:407
  2.9 131.3 %shard_map.46 = bf16[1,512,896]{2,1,0:T(8,128)(2,1)} custom-call(bf16[64,5120]{1,0:T(8,128)(2,1)} %tok_ref.1, f32[160,1]{1,0:T(8,128)} %copy.5.gain_ref, f32[160,7168]{1,0:T(8,128)} %w_ref.1, f32[7,128]{1,0:T(8,128)} %tile.12.bias_ref), custom_call_target="tpu_custom_call" | custom-call | tf_op jit(solution)/shard_map/pallas_call | solution.py:384
  134.2 2.2 %copy.7 = bf16[1,512,896]{2,1,0:T(8,128)(2,1)} copy(bf16[1,512,896]{2,1,0:T(8,128)(2,1)} %shard_map.46) | data formatting | bytes 1835008
  (1 shorter events, 0.0 us)

commit v2 on v1

--- a/solution.py
+++ b/solution.py
@@ -137,18 +137,6 @@
             device_id_type=MESH,
         )
 
-    gain = gain_ref[...].astype(jnp.bfloat16).astype(jnp.float32)
-    query = QHEADS * HEAD_DIM // TP
-    pair = KVHEADS * HEAD_DIM // TP
-    for rank in range(TP):
-        starts = (
-            (rank * query, 0, query),
-            (TP * query + rank * pair, query, pair),
-            (TP * (query + pair) + rank * pair, query + pair, pair),
-        )
-        for source, target, extent in starts:
-            part = w_ref[:, source : source + extent].astype(jnp.bfloat16).astype(jnp.float32)
-            wsend[rank, :, target : target + extent] = (part * gain).astype(jnp.bfloat16)
     for piece in range(pieces):
         tbuf[me * pieces + piece] = tok_ref[piece * piece_rows : (piece + 1) * piece_rows, :]
     bbuf[flat] = bias_ref[...]
@@ -210,11 +198,23 @@
         each(z < line - 1, lambda piece=piece: own_token_copy(piece, 0, up).start())
         each(z > 0, lambda piece=piece: own_token_copy(piece, 1, down).start())
         own_token_copy(piece, 2, y_peer).start()
+    gain = gain_ref[...].astype(jnp.bfloat16).astype(jnp.float32)
+    query = QHEADS * HEAD_DIM // TP
+    pair = KVHEADS * HEAD_DIM // TP
+    for rank in range(TP):
+        starts = (
+            (rank * query, 0, query),
+            (TP * query + rank * pair, query, pair),
+            (TP * (query + pair) + rank * pair, query + pair, pair),
+        )
+        for source, target, extent in starts:
+            part = w_ref[:, source : source + extent].astype(jnp.bfloat16).astype(jnp.float32)
+            wsend[rank, :, target : target + extent] = (part * gain).astype(jnp.bfloat16)
     core_copy(0, inst, 0).start()
     x_copy(0).start()
-    order = (7, 6, 5, 4, 3, 2, 1)
-    for k in order:
-        all_gather_copy(k).start()
+    all_gather_copy(1).start()
+    all_gather_copy(2).start()
+    all_gather_copy(3).start()
 
     def bias_copy(step):
         there = lax.rem(flat + step, devices)
@@ -277,19 +277,27 @@
         )
 
     relay_hop(1)
+    all_gather_copy(4).start()
+    all_gather_copy(5).start()
+    all_gather_copy(6).start()
+    all_gather_copy(7).start()
     relay_x(0)
-    for k in order[:3]:
-        relay_weight(k)
+    relay_weight(1)
+    relay_weight(2)
+    relay_weight(3)
     relay_hop(2)
-    for k in order[3:5]:
-        relay_weight(k)
-    for k in order[:2]:
-        relay_x(k)
+    relay_weight(4)
+    relay_weight(5)
     relay_hop(3)
-    for k in order[5:]:
-        relay_weight(k)
-    for k in order[2:]:
-        relay_x(k)
+    relay_x(1)
+    relay_x(2)
+    relay_weight(6)
+    relay_weight(7)
+    relay_x(3)
+    relay_x(4)
+    relay_x(5)
+    relay_x(6)
+    relay_x(7)
 
     for k in range(shard_count):
         wait_block(core_peer * shard_count + mate(k))

time: 137 us -> 123 us (0.90)
  the two profiles are of different devices: /device:TPU:11 before, /device:TPU:0 now
where the time goes in v2:
time: 123 us; the launch traced here: 122 us
  Pallas kernels  117 us (95%)
  local copies, waits for them, and re-layouts  5.03 us (4%)
    pallas_call x1, Pallas kernels, kernel_device(): pl.pallas_call(functools.partial(kernel, dims), out_shape=jax.ShapeDtypeS...  117 us

profile of v2, /device:TPU:0, one launch (start us, length us, event | category | flops | bytes accessed | tf_op | source)
XLA Modules:
  0.0 121.6 jit_solution(5541677318965233423)
XLA Ops:
  0.0 0.8 tile.10
  0.8 0.7 tile.12.bias_ref
  1.4 1.4 %copy.5.gain_ref = f32[160,1]{1,0:T(8,128)} copy(f32[160,1]{0,1:T(1,128)} %bitcast.1) | data formatting | bytes 1280 | tf_op jit(solution)/shard_map/reshape | solution.py:415
  2.9 116.6 %shard_map.46 = bf16[1,512,896]{2,1,0:T(8,128)(2,1)} custom-call(bf16[64,5120]{1,0:T(8,128)(2,1)} %tok_ref.1, f32[160,1]{1,0:T(8,128)} %copy.5.gain_ref, f32[160,7168]{1,0:T(8,128)} %w_ref.1, f32[7,128]{1,0:T(8,128)} %tile.12.bias_ref), custom_call_target="tpu_custom_call" | custom-call | tf_op jit(solution)/shard_map/pallas_call | solution.py:392
  119.4 2.2 %copy.7 = bf16[1,512,896]{2,1,0:T(8,128)(2,1)} copy(bf16[1,512,896]{2,1,0:T(8,128)(2,1)} %shard_map.46) | data formatting | bytes 1835008
  (1 shorter events, 0.0 us)
